TPU v7x, 128 devices: a whole 4x4x4 slice. The times are simulated.
128 devices in a mesh: group: 4 (over y_hi, core), patch: 32 (over y_lo, x, z).
Axes of the slice: x: 4, y: 4 (y_hi: 2, y_lo: 2; y = y_hi * 2 + y_lo), z: 4, core: 2. Of those that a mesh axis runs over, the one named last changes fastest.
Arguments:
- fine_nodes: bfloat16 [131072, 512], P(('group', 'patch')), may hold values from -6 to 6
- coarse_nodes: bfloat16 [2048, 512], P(('group', 'patch')), may hold values from -6 to 6
- fine_edges: bfloat16 [524288, 512], P(('group', 'patch')), may hold values from -6 to 6
- fine_senders: int32 [524288], P(('group', 'patch')), may hold values from 0 to 1279
- fine_receivers: int32 [524288], P(('group', 'patch')), may hold values from 0 to 1023
- fine_live: int32 [128], P(('group', 'patch')), may hold values from 128 to 4096, as said below
- up_edges: bfloat16 [65536, 512], P(('group', 'patch')), may hold values from -6 to 6
- up_senders: int32 [65536], P(('group', 'patch')), may hold values from 0 to 1023
- up_receivers: int32 [65536], P(('group', 'patch')), may hold values from 0 to 2047
- down_edges: bfloat16 [65536, 512], P(('group', 'patch')), may hold values from -6 to 6
- down_senders: int32 [65536], P(('group', 'patch')), may hold values from 0 to 2047
- down_receivers: int32 [65536], P(('group', 'patch')), may hold values from 0 to 1023
- edge_in_weight: bfloat16 [1536, 512], replicated, may hold values from -0.15625 to 0.15625
- edge_in_bias: float32 [512], replicated, may hold values from -3 to 3
- edge_out_weight: bfloat16 [512, 512], replicated, may hold values from -0.25 to 0.25
- edge_out_bias: float32 [512], replicated, may hold values from -3 to 3
- edge_gain: float32 [512], replicated, may hold values from 0.25 to 1.75
- edge_shift: float32 [512], replicated, may hold values from -2 to 2
- node_in_weight: bfloat16 [1024, 512], replicated, may hold values from -0.1875 to 0.1875
- node_in_bias: float32 [512], replicated, may hold values from -3 to 3
- node_out_weight: bfloat16 [512, 512], replicated, may hold values from -0.25 to 0.25
- node_out_bias: float32 [512], replicated, may hold values from -3 to 3
- node_gain: float32 [512], replicated, may hold values from 0.25 to 1.75
- node_shift: float32 [512], replicated, may hold values from -2 to 2
Outputs:
- fine_out: bfloat16 [131072, 512], P(('group', 'patch'))
- coarse_out: bfloat16 [2048, 512], P(('group', 'patch'))
- fine_edges_out: bfloat16 [524288, 512], P(('group', 'patch'))
- up_edges_out: bfloat16 [65536, 512], P(('group', 'patch'))
- down_edges_out: bfloat16 [65536, 512], P(('group', 'patch'))
Inputs may be any that keep to these rules, and one draw needn't show every extreme that they name: `fine_live`: a multiple of 128; some patch has all 4096 slots live in every draw.
All inputs are finite; a program needn't handle non-finite values.
Results may differ from a plain program's by a relative error of at most 0.0049.
Values may be sent and summed in bfloat16 or wider, within the bound.
A program may use at most 128 MiB of HBM per device.

v0:
```python
import jax
import jax.numpy as jnp
from jax import lax
from jax.sharding import PartitionSpec as P

RIM = 128


def extended(shard, sides, width):
    for axis, dim in sides:
        size, length = (lax.axis_size(axis), shard.shape[dim])
        up = [(i, (i + 1) % size) for i in range(size)]
        down = [(j, i) for i, j in up]
        last = lax.slice_in_dim(shard, length - width, length, axis=dim)
        first = lax.slice_in_dim(shard, 0, width, axis=dim)
        before = lax.ppermute(last, axis, up)
        after = lax.ppermute(first, axis, down)
        shard = jnp.concatenate([before, shard, after], axis=dim)
    return shard


def split_up(shard, dim, size):
    lengths = shard.shape
    parts = shard.reshape(*lengths[:dim], size, lengths[dim] // size, *lengths[dim + 1 :])
    return jnp.moveaxis(parts, dim, 0)


def sent_and_summed(shard, axis, dim):
    size = lax.axis_size(axis)
    parts = lax.all_to_all(split_up(shard, dim, size), axis, 0, 0, tiled=True)
    return jnp.sum(parts, axis=0)


def perceptron(inputs, in_weight, in_bias, out_weight, out_bias, gain, shift):
    preact = jnp.dot(inputs, in_weight, preferred_element_type=jnp.float32) + in_bias
    hidden = jax.nn.silu(preact).astype(jnp.bfloat16)
    result = jnp.dot(hidden, out_weight, preferred_element_type=jnp.float32) + out_bias
    average = jnp.mean(result, axis=-1, keepdims=True)
    centred = result - average
    spread = jnp.mean(centred * centred, axis=-1, keepdims=True)
    return centred * lax.rsqrt(spread + 1e-05) * gain + shift


def body(
    fine_nodes,
    coarse_nodes,
    fine_edges,
    fine_senders,
    fine_receivers,
    fine_live,
    up_edges,
    up_senders,
    up_receivers,
    down_edges,
    down_senders,
    down_receivers,
    edge_in_weight,
    edge_in_bias,
    edge_out_weight,
    edge_out_bias,
    edge_gain,
    edge_shift,
    node_in_weight,
    node_in_bias,
    node_out_weight,
    node_out_bias,
    node_gain,
    node_shift,
):
    edge_params = (
        edge_in_weight,
        edge_in_bias,
        edge_out_weight,
        edge_out_bias,
        edge_gain,
        edge_shift,
    )
    node_params = (
        node_in_weight,
        node_in_bias,
        node_out_weight,
        node_out_bias,
        node_gain,
        node_shift,
    )
    node_count = fine_nodes.shape[0]
    fine_slots = fine_edges.shape[0]
    up_count = up_edges.shape[0]
    window = extended(fine_nodes, (("patch", 0),), RIM)
    gathered = lax.all_gather(coarse_nodes, ("group", "patch"), axis=0, tiled=True)
    coarse_count = gathered.shape[0]
    fine_in = jnp.concatenate(
        [fine_edges, window[fine_senders], fine_nodes[fine_receivers]], axis=1
    )
    up_in = jnp.concatenate([up_edges, fine_nodes[up_senders], gathered[up_receivers]], axis=1)
    down_in = jnp.concatenate(
        [down_edges, gathered[down_senders], fine_nodes[down_receivers]], axis=1
    )
    all_edges = jnp.concatenate([fine_edges, up_edges, down_edges], axis=0).astype(jnp.float32)
    updated = all_edges + perceptron(
        jnp.concatenate([fine_in, up_in, down_in], axis=0), *edge_params
    )
    live_mask = (jnp.arange(fine_slots) < fine_live[0])[:, None]
    fine_new = jnp.where(live_mask, updated[:fine_slots], all_edges[:fine_slots])
    up_new = updated[fine_slots : fine_slots + up_count]
    down_new = updated[fine_slots + up_count :]
    fine_sum = jax.ops.segment_sum(
        jnp.where(live_mask, fine_new, 0.0), fine_receivers, num_segments=node_count
    )
    fine_sum = (
        fine_sum + jax.ops.segment_sum(down_new, down_receivers, num_segments=node_count)
    ).astype(jnp.bfloat16)
    fine_out = fine_nodes.astype(jnp.float32) + perceptron(
        jnp.concatenate([fine_nodes, fine_sum], axis=1), *node_params
    )
    owned_count = coarse_nodes.shape[0]
    groups = lax.axis_size("group")
    patches = lax.axis_size("patch")
    partial_value = jax.ops.segment_sum(up_new, up_receivers, num_segments=coarse_count)
    partial_value = partial_value.reshape(groups, patches, owned_count, partial_value.shape[1])
    section_one = sent_and_summed(partial_value, "group", 0)
    coarse_total = sent_and_summed(section_one, "patch", 1).reshape(
        owned_count, partial_value.shape[3]
    )
    coarse_sum = coarse_total.astype(jnp.bfloat16)
    coarse_out = coarse_nodes.astype(jnp.float32) + perceptron(
        jnp.concatenate([coarse_nodes, coarse_sum], axis=1), *node_params
    )
    return (
        fine_out.astype(jnp.bfloat16),
        coarse_out.astype(jnp.bfloat16),
        fine_new.astype(jnp.bfloat16),
        up_new.astype(jnp.bfloat16),
        down_new.astype(jnp.bfloat16),
    )


def solution(mesh):
    return jax.shard_map(
        body,
        mesh=mesh,
        in_specs=(
            P(("group", "patch"), None),
            P(("group", "patch"), None),
            P(("group", "patch"), None),
            P(("group", "patch")),
            P(("group", "patch")),
            P(("group", "patch")),
            P(("group", "patch"), None),
            P(("group", "patch")),
            P(("group", "patch")),
            P(("group", "patch"), None),
            P(("group", "patch")),
            P(("group", "patch")),
            P(),
            P(),
            P(),
            P(),
            P(),
            P(),
            P(),
            P(),
            P(),
            P(),
            P(),
            P(),
        ),
        out_specs=(
            P(("group", "patch"), None),
            P(("group", "patch"), None),
            P(("group", "patch"), None),
            P(("group", "patch"), None),
            P(("group", "patch"), None),
        ),
        check_vma=False,
    )
```

profile of v0, /device:TPU:1, one launch (start us, length us, event | category | flops | bytes accessed | tf_op | source)
XLA Modules:
  0.0 490.3 jit_solution(15975151159262812078)
XLA Ops:
  7.2 0.0 copy-start
  7.2 0.0 all-gather.2.cloned.1.call-start
  7.2 0.7 all-gather.2.cloned.1.call-update
  7.9 1.6 fusion.63
  9.5 2.5 collective-permute-start
  12.0 5.3 %collective-permute-start.1 = (bf16[128,512]{1,0:T(8,128)(2,1)S(1)}, bf16[128,512]{1,0:T(8,128)(2,1)S(1)}, u32[]{:S(2)}, u32[]{:S(2)}) collective-permute-start(bf16[128,512]{1,0:T(8,128)(2,1)S(1)} %get-tuple-element.25), channel_id=1, source_target_pairs={{1,0},{2,1},{3,2},{4,3},{5,4},{6,5},{7,6},{8,7},{9,8},{10,9},{11,1... | collective-permute-start | bytes 393224 | tf_op jit(solution)/shard_map/ppermute | solution.py:17
  17.3 1.3 copy.50
  18.6 2.0 copy.51
  20.7 0.0 copy-start.11
  20.7 0.0 copy-start.12
  20.7 6.4 %copy.49 = bf16[4096,512]{0,1:T(8,128)(2,1)} copy(bf16[4096,512]{1,0:T(8,128)(2,1)} %param.26) | data formatting | bytes 8388608 | tf_op args[2]
  27.1 0.6 pad_clamp_fusion.3
  27.7 0.6 pad_clamp_fusion.1
  28.3 0.6 pad_clamp_fusion.2
  28.9 0.6 fusion.49
  29.5 6.6 %maximum_convert_fusion = f32[5120,512]{0,1:T(8,128)} fusion(bf16[512,512]{0,1:T(8,128)(2,1)} %copy.51, bf16[512,512]{0,1:T(8,128)(2,1)S(1)} %copy.50, bf16[4096,512]{0,1:T(8,128)(2,1)} %copy.49), kind=kLoop, calls=%fused_computation.32 | loop fusion | flops 15728640 | bytes 15728640 | tf_op jit(solution)/shard_map/convert_element_type | solution.py:99
  36.1 0.6 pad_clamp_fusion
  36.7 1.3 copy.48
  38.7 2.8 gather_fusion.5
  41.5 2.7 gather_fusion.2
  44.2 18.5 %gather_fusion.1 = bf16[4096,512]{1,0:T(8,128)(2,1)} fusion(bf16[1024,512]{1,0:T(8,128)(2,1)S(1)} %copy-done.2, s32[4096]{0:T(1024)} %fusion.49), kind=kCustom, calls=%fused_computation.1 | custom fusion | bytes 8404992 | tf_op jit(solution)/shard_map/gather | solution.py:93
  62.7 0.6 iota_compare_fusion
  63.3 1.2 pad_maximum_fusion
  64.6 18.9 %gather_fusion = bf16[4096,512]{1,0:T(8,128)(2,1)} fusion(bf16[1280,512]{1,0:T(8,128)(2,1)} %pad_maximum_fusion, s32[4096]{0:T(1024)S(1)} %fusion.48), kind=kCustom, calls=%fused_computation | custom fusion | bytes 8404992 | tf_op jit(solution)/shard_map/gather | solution.py:93
  83.5 232.3 %all-gather.2.cloned.1.call-done = bf16[2048,512]{1,0:T(8,128)(2,1)} async-done(((bf16[16,512]{1,0:T(8,128)(2,1)}), bf16[2048,512]{1,0:T(8,128)(2,1)}) %all-gather.2.cloned.1.call-update) | async-done | bytes 2097168 | tf_op jit(solution)/shard_map/all_gather | solution.py:90
  315.8 4.5 gather_fusion.3
  320.3 4.5 gather_fusion.4
  324.9 0.0 copy-start.25
  324.9 27.5 %multiply_convert_fusion.clone.1.clone.4 = bf16[5120,512]{1,0:T(8,128)(2,1)} fusion(bf16[1536,512]{1,0:T(8,128)(2,1)S(1)} %copy-done, bf16[512,512]{1,0:T(8,128)(2,1)} %gather_fusion.5, bf16[512,512]{1,0:T(8,128)(2,1)} %gather_fusion.4, bf16[512,512]{1,0:T(8,128)(2,1)} %param.33, bf16[512,512]{1,0:T(8,128)(2,1)} %gather_fusion.3, ...), kind=kOutput, calls=%fused_computation.29.clone.clone.clone.clone.clone.1 | convolution fusion | flops 8210350080 | bytes 22546432 | tf_op jit(solution)/shard_map/dot_general | solution.py:35
  352.4 5.3 %add_reduce_fusion = (f32[5120]{0:T(1024)S(1)}, f32[5120,512]{0,1:T(8,128)S(1)}) fusion(f32[512]{0:T(512)S(1)} %copy-done.17, bf16[512,512]{1,0:T(8,128)(2,1)S(1)} %copy-done.25, bf16[5120,512]{1,0:T(8,128)(2,1)} %multiply_convert_fusion.clone.1.clone.4), kind=kOutput, calls=%fused_computation.30 | convolution fusion | flops 2689592320 | bytes 16275456 | tf_op jit(solution)/shard_map/dot_general | solution.py:37
  357.7 0.0 copy-start.23
  357.7 0.0 copy-start.24
  357.7 1.9 multiply_reduce_fusion
  359.7 0.2 copy-done.4
  359.9 0.1 copy-done.5
  360.0 3.1 add_add_fusion
  363.1 3.8 copy-done.3
  366.9 1.1 fusion.62
  368.0 2.5 copy.54
  370.5 6.5 %scatter_custom_fusion.2 = f32[2048,512]{1,0:T(8,128)} fusion(s32[512]{0:T(512)} %param.32, f32[512,512]{1,0:T(8,128)} %copy.54, f32[]{:T(128)} %constant.9.clone.1), kind=kCustom, calls=%fused_computation.40 | custom fusion | flops 262144 | bytes 4194816 | tf_op jit(solution)/shard_map/scatter-add | solution.py:119
  377.0 5.2 %all-to-all-start = ((f32[4,1,32,16,512]{4,3,2,1,0:T(8,128)}), f32[4,1,32,16,512]{4,3,2,1,0:T(8,128)}, u32[]{:S(2)}, u32[]{:S(2)}) async-start(f32[4,1,32,16,512]{4,3,2,1,0:T(8,128)} %bitcast.17), calls=%async_computation | async-start | bytes 8388608 | tf_op jit(solution)/shard_map/all_to_all | solution.py:30
  382.2 9.5 %broadcast_select_fusion = f32[4096,512]{0,1:T(8,128)} fusion(pred[4096]{0:T(1024)(128)(4,1)S(1)} %copy-done.9, f32[5120,512]{0,1:T(8,128)} %maximum_convert_fusion, f32[5120,512]{0,1:T(8,128)} %copy-done.3), kind=kLoop, calls=%fused_computation.34 | loop fusion | flops 4194304 | bytes 25169920 | tf_op jit(solution)/shard_map/jit(_where)/select_n | solution.py:108
  391.7 1.4 copy.53
  393.1 5.7 %scatter_custom_fusion.1 = f32[1024,512]{1,0:T(8,128)} fusion(s32[512]{0:T(512)} %param.35, f32[512,512]{1,0:T(8,128)} %copy.53, f32[]{:T(128)} %constant.9.clone.1), kind=kCustom, calls=%fused_computation.53 | custom fusion | flops 262144 | bytes 2097664 | tf_op jit(solution)/shard_map/scatter-add | solution.py:111
  398.8 9.1 %copy.52 = f32[4096,512]{1,0:T(8,128)} copy(f32[4096,512]{0,1:T(8,128)} %broadcast_select_fusion) | data formatting | bytes 16777216 | tf_op jit(solution)/shard_map/jit(_where)/select_n | solution.py:108
  407.8 26.6 %scatter_custom_fusion = f32[1024,512]{1,0:T(8,128)} fusion(s32[4096]{0:T(1024)} %param.28, f32[4096,512]{1,0:T(8,128)} %copy.52, f32[]{:T(128)} %constant.9.clone.1), kind=kCustom, calls=%fused_computation.55 | custom fusion | flops 2097152 | bytes 2097664 | tf_op jit(solution)/shard_map/scatter-add | solution.py:107
  434.5 2.6 add_convert_fusion.1
  437.1 4.6 add_reduce_fusion.1
  441.7 8.3 %fusion.23 = bf16[4096,512]{0,1:T(8,128)(2,1)} fusion(f32[5120,512]{0,1:T(8,128)} %maximum_convert_fusion, f32[5120,512]{0,1:T(8,128)} %copy-done.3, pred[4096]{0:T(1024)(128)(4,1)S(1)} %copy-done.9), kind=kLoop, calls=%fused_computation.35 | loop fusion | flops 2097152 | bytes 12587008 | tf_op jit(solution)/shard_map/convert_element_type | solution.py:132
  450.0 3.7 reduce_sum.76
  453.8 7.9 %all-to-all-start.1 = ((f32[32,1,1,16,512]{4,3,2,1,0:T(8,128)}), f32[32,1,1,16,512]{4,3,2,1,0:T(8,128)}, u32[]{:S(2)}, u32[]{:S(2)}) async-start(f32[32,1,1,16,512]{4,3,2,1,0:T(8,128)} %bitcast.3), calls=%async_computation.1 | async-start | bytes 2097152 | tf_op jit(solution)/shard_map/all_to_all | solution.py:30
  461.7 1.7 fusion.61
  463.4 1.0 copy.59
  464.4 1.0 copy.58
  465.4 6.5 %copy.57 = bf16[4096,512]{1,0:T(8,128)(2,1)} copy(bf16[4096,512]{0,1:T(8,128)(2,1)} %fusion.23) | data formatting | bytes 8388608
  471.9 1.9 multiply_reduce_fusion.1
  473.8 0.0 copy-start.8
  473.8 0.0 copy-start.1
  473.9 3.3 add_convert_fusion
  477.2 2.3 copy.56
  479.5 1.3 reduce_sum.77
  480.8 1.7 fusion.68
  482.5 0.2 multiply_reduce_fusion.2
  482.7 0.7 add_convert_fusion.2
  (58 shorter events, 0.1 us)
Async XLA Ops:
  7.2 317.7 %copy-start = (bf16[1536,512]{1,0:T(8,128)(2,1)S(1)}, bf16[1536,512]{1,0:T(8,128)(2,1)}, u32[]{:S(2)}) copy-start(bf16[1536,512]{1,0:T(8,128)(2,1)} %param.36) | copy-start | bytes 4718596
  7.2 308.6 %all-gather.2.cloned.1.call-start = ((), (), s32[]{:S(2)}) async-start(), calls=%async_computation.2 | async-start | bytes 2113536 | tf_op jit(solution)/shard_map/all_gather | solution.py:90
  9.5 53.8 %collective-permute-start = (bf16[128,512]{1,0:T(8,128)(2,1)}, bf16[128,512]{1,0:T(8,128)(2,1)S(1)}, u32[]{:S(2)}, u32[]{:S(2)}) collective-permute-start(bf16[128,512]{1,0:T(8,128)(2,1)} %get-tuple-element.24), channel_id=1, source_target_pairs={{0,1},{1,2},{2,3},{3,4},{4,5},{5,6},{6,7},{7,8},{8,9},{9,10},{10,1... | collective-permute-start | bytes 393224 | tf_op jit(solution)/shard_map/ppermute | solution.py:16
  12.0 51.3 %collective-permute-start.1 = (bf16[128,512]{1,0:T(8,128)(2,1)S(1)}, bf16[128,512]{1,0:T(8,128)(2,1)S(1)}, u32[]{:S(2)}, u32[]{:S(2)}) collective-permute-start(bf16[128,512]{1,0:T(8,128)(2,1)S(1)} %get-tuple-element.25), channel_id=1, source_target_pairs={{1,0},{2,1},{3,2},{4,3},{5,4},{6,5},{7,6},{8,7},{9,8},{10,9},{11,1... | collective-permute-start | bytes 393224 | tf_op jit(solution)/shard_map/ppermute | solution.py:17
  20.6 6.4 %copy-start.19 = (s32[512]{0:T(512)S(1)}, s32[512]{0:T(512)}, u32[]{:S(2)}) copy-start(s32[512]{0:T(512)} %param.31) | copy-start | bytes 6148
  20.6 7.0 %copy-start.20 = (s32[512]{0:T(512)S(1)}, s32[512]{0:T(512)}, u32[]{:S(2)}) copy-start(s32[512]{0:T(512)} %param.34) | copy-start | bytes 6148
  20.6 7.6 %copy-start.21 = (s32[512]{0:T(512)S(1)}, s32[512]{0:T(512)}, u32[]{:S(2)}) copy-start(s32[512]{0:T(512)} %param.32) | copy-start | bytes 6148
  20.6 8.2 %copy-start.22 = (s32[512]{0:T(512)S(1)}, s32[512]{0:T(512)}, u32[]{:S(2)}) copy-start(s32[512]{0:T(512)} %param.35) | copy-start | bytes 6148
  20.7 8.2 %copy-start.11 = (s32[4096]{0:T(1024)S(1)}, s32[4096]{0:T(1024)}, u32[]{:S(2)}) copy-start(s32[4096]{0:T(1024)} %param.27) | copy-start | bytes 49156
  20.7 8.2 %copy-start.12 = (s32[4096]{0:T(1024)S(1)}, s32[4096]{0:T(1024)}, u32[]{:S(2)}) copy-start(s32[4096]{0:T(1024)} %param.28) | copy-start | bytes 49156
  29.5 7.2 %copy-start.2 = (bf16[1024,512]{1,0:T(8,128)(2,1)S(1)}, bf16[1024,512]{1,0:T(8,128)(2,1)}, u32[]{:S(2)}) copy-start(bf16[1024,512]{1,0:T(8,128)(2,1)} %param.24) | copy-start | bytes 3145732
  64.6 251.2 %copy-start.14 = (s32[1024]{0:T(1024)S(1)}, s32[1024]{0:T(1024)}, u32[]{:S(2)}) copy-start(s32[1024]{0:T(1024)} %pad_clamp_fusion.2) | copy-start | bytes 12292
  83.4 236.9 %copy-start.13 = (s32[1024]{0:T(1024)S(1)}, s32[1024]{0:T(1024)}, u32[]{:S(2)}) copy-start(s32[1024]{0:T(1024)} %pad_clamp_fusion.1) | copy-start | bytes 12292
  83.5 241.4 %copy-start.26 = (f32[512]{0:T(512)S(1)}, f32[512]{0:T(512)}, u32[]{:S(2)}) copy-start(f32[512]{0:T(512)} %param.37) | copy-start | bytes 6148
  324.9 27.5 %copy-start.17 = (f32[512]{0:T(512)S(1)}, f32[512]{0:T(512)}, u32[]{:S(2)}) copy-start(f32[512]{0:T(512)} %param.39) | copy-start | bytes 6148
  324.9 27.5 %copy-start.25 = (bf16[512,512]{1,0:T(8,128)(2,1)S(1)}, bf16[512,512]{1,0:T(8,128)(2,1)}, u32[]{:S(2)}) copy-start(bf16[512,512]{1,0:T(8,128)(2,1)} %param.38) | copy-start | bytes 1572868
  357.7 2.2 copy-start.4
  357.7 2.3 copy-start.5
  357.7 2.3 copy-start.23
  357.7 2.3 copy-start.24
  363.1 3.8 copy-start.3
  377.0 5.2 %copy-start.9 = (pred[4096]{0:T(1024)(128)(4,1)S(1)}, pred[4096]{0:T(1024)(128)(4,1)}, u32[]{:S(2)}) copy-start(pred[4096]{0:T(1024)(128)(4,1)} %iota_compare_fusion) | copy-start | bytes 12292
  377.0 73.0 %all-to-all-start = ((f32[4,1,32,16,512]{4,3,2,1,0:T(8,128)}), f32[4,1,32,16,512]{4,3,2,1,0:T(8,128)}, u32[]{:S(2)}, u32[]{:S(2)}) async-start(f32[4,1,32,16,512]{4,3,2,1,0:T(8,128)} %bitcast.17), calls=%async_computation | async-start | bytes 8388608 | tf_op jit(solution)/shard_map/all_to_all | solution.py:30
  407.8 29.2 %copy-start.7 = (bf16[512,512]{1,0:T(8,128)(2,1)S(1)}, bf16[512,512]{1,0:T(8,128)(2,1)}, u32[]{:S(2)}) copy-start(bf16[512,512]{1,0:T(8,128)(2,1)} %param.44) | copy-start | bytes 1572868
  407.8 29.2 %copy-start.10 = (f32[512]{0:T(512)S(1)}, f32[512]{0:T(512)}, u32[]{:S(2)}) copy-start(f32[512]{0:T(512)} %param.45) | copy-start | bytes 6148
  407.8 29.2 %copy-start.18 = (f32[512]{0:T(512)S(1)}, f32[512]{0:T(512)}, u32[]{:S(2)}) copy-start(f32[512]{0:T(512)} %param.43) | copy-start | bytes 6148
  453.8 25.7 %all-to-all-start.1 = ((f32[32,1,1,16,512]{4,3,2,1,0:T(8,128)}), f32[32,1,1,16,512]{4,3,2,1,0:T(8,128)}, u32[]{:S(2)}, u32[]{:S(2)}) async-start(f32[32,1,1,16,512]{4,3,2,1,0:T(8,128)} %bitcast.3), calls=%async_computation.1 | async-start | bytes 2097152 | tf_op jit(solution)/shard_map/all_to_all | solution.py:30
  465.4 8.5 %copy-start.6 = (bf16[1024,512]{0,1:T(8,128)(2,1)S(1)}, bf16[1024,512]{0,1:T(8,128)(2,1)}, u32[]{:S(2)}) copy-start(bf16[1024,512]{0,1:T(8,128)(2,1)} %copy.48) | copy-start | bytes 3145732
  465.4 8.5 %copy-start.15 = (f32[512]{0:T(512)S(1)}, f32[512]{0:T(512)}, u32[]{:S(2)}) copy-start(f32[512]{0:T(512)} %param.47) | copy-start | bytes 6148
  465.4 8.5 %copy-start.16 = (f32[512]{0:T(512)S(1)}, f32[512]{0:T(512)}, u32[]{:S(2)}) copy-start(f32[512]{0:T(512)} %param.46) | copy-start | bytes 6148
  473.8 7.0 %copy-start.8 = (bf16[16,512]{1,0:T(8,128)(2,1)S(1)}, bf16[16,512]{1,0:T(8,128)(2,1)}, u32[]{:S(2)}) copy-start(bf16[16,512]{1,0:T(8,128)(2,1)} %param.25) | copy-start | bytes 49156
  473.8 9.6 %copy-start.1 = (bf16[1536,512]{1,0:T(8,128)(2,1)S(1)}, bf16[1536,512]{1,0:T(8,128)(2,1)}, u32[]{:S(2)}) copy-start(bf16[1536,512]{1,0:T(8,128)(2,1)} %param.36) | copy-start | bytes 4718596
Sparse Core Ops, SparseCore 0:
  9.7 306.0 all-gather.1
where the time goes:
time: 492 us; the launch traced here: 490 us
  waiting for transfers between devices  233 us (47%)
  local copies, waits for them, and re-layouts  95.4 us (19%)
  other arithmetic  86.8 us (18%)
  matrix products  39.1 us (8%)
  starting transfers between devices  20.9 us (4%)
  between operations  15 us (3%)
    all_gather x1, waiting for transfers between devices, body(): lax.all_gather(coarse_nodes, ('group', 'patch'), axis=0, tiled=True)  232 us
    dot_general x1, matrix products, perceptron(): jnp.dot(inputs, in_weight, preferred_element_type=jnp.float32) + in_bias  27.5 us
    scatter-add x1, other arithmetic, body(): jax.ops.segment_sum(jnp.where(live_mask, fine_new, 0.0), fine_receivers,...  26.6 us
    unnamed x62, local copies, waits for them, and re-layouts  26 us
    gather x1, local copies, waits for them, and re-layouts, body(): window[fine_senders]  18.9 us
    gather x1, local copies, waits for them, and re-layouts, body(): fine_nodes[fine_receivers]  18.5 us
    all_to_all x2, starting transfers between devices, sent_and_summed(): parts = lax.all_to_all(split_up(shard, dim, size), axis, 0, 0, tiled=True)  13 us
    dot_general x3, matrix products, perceptron(): jnp.dot(hidden, out_weight, preferred_element_type=jnp.float32) + out_bias  11.7 us
  transfers between devices with their start and end apart: 5, of which 1 were waited for; matrix products, arithmetic and copies ran while one was open for 31% of the time, Pallas kernels for 0%

commit v1 on v0

--- a/solution.py
+++ b/solution.py
@@ -87,7 +87,14 @@
     fine_slots = fine_edges.shape[0]
     up_count = up_edges.shape[0]
     window = extended(fine_nodes, (("patch", 0),), RIM)
-    gathered = lax.all_gather(coarse_nodes, ("group", "patch"), axis=0, tiled=True)
+
+    def keep_up_stacks_all(q_in, axis_key):
+        spare = lax.axis_size(axis_key)
+        outcome_arr = jnp.stack(spare * [q_in])
+        piece_now = lax.all_to_all(outcome_arr, axis_key, concat_axis=0, split_axis=0)
+        return jnp.concatenate(piece_now, axis=0)
+
+    gathered = keep_up_stacks_all(coarse_nodes, ("group", "patch"))
     coarse_count = gathered.shape[0]
     fine_in = jnp.concatenate(
         [fine_edges, window[fine_senders], fine_nodes[fine_receivers]], axis=1

time: 492 us -> 254 us (0.52)
  waiting for transfers between devices: 233 us -> 0.01 us
  between operations: 15 us -> 1.66 us
  starting transfers between devices: 20.9 us -> 28 us
    all_gather x1 -> x0, waiting for transfers between devices: 232 us -> none  [body(): lax.all_gather(coarse_nodes, ('group', 'patch'), axis=0, tiled=True)]
    all_to_all x0 -> x1, starting transfers between devices: none -> 6.18 us  [keep_up_stacks_all(): lax.all_to_all(outcome_arr, axis_key, concat_axis=0, split_axis=0)]
    unnamed x62 -> x66, local copies, waits for them, and re-layouts: 26 us -> 23.9 us
  transfers between devices with their start and end apart: 5 -> 5, of which waited for: 1 -> 0; matrix products, arithmetic and copies ran while one was open for 31% -> 60% of each run, Pallas kernels for 0% -> 0%
where the time goes in v1:
time: 254 us; the launch traced here: 252 us
  local copies, waits for them, and re-layouts  96 us (38%)
  other arithmetic  87 us (34%)
  matrix products  39.1 us (15%)
  starting transfers between devices  28 us (11%)
    dot_general x1, matrix products, perceptron(): jnp.dot(inputs, in_weight, preferred_element_type=jnp.float32) + in_bias  27.5 us
    scatter-add x1, other arithmetic, body(): jax.ops.segment_sum(jnp.where(live_mask, fine_new, 0.0), fine_receivers,...  26.6 us
    unnamed x66, local copies, waits for them, and re-layouts  23.9 us
    gather x1, local copies, waits for them, and re-layouts, body(): window[fine_senders]  19 us
    gather x1, local copies, waits for them, and re-layouts, body(): fine_nodes[fine_receivers]  18.6 us
    all_to_all x2, starting transfers between devices, sent_and_summed(): parts = lax.all_to_all(split_up(shard, dim, size), axis, 0, 0, tiled=True)  14 us
    dot_general x3, matrix products, perceptron(): jnp.dot(hidden, out_weight, preferred_element_type=jnp.float32) + out_bias  11.7 us
    select_n x1, other arithmetic, body(): jnp.where(live_mask, fine_new, 0.0)  9.46 us
  transfers between devices with their start and end apart: 5, of which 0 were waited for; matrix products, arithmetic and copies ran while one was open for 60% of the time, Pallas kernels for 0%

profile of v1, /device:TPU:1, one launch (start us, length us, event | category | flops | bytes accessed | tf_op | source)
XLA Modules:
  0.0 251.8 jit_solution(2462989248531562432)
XLA Ops:
  0.6 0.0 copy-start
  0.7 0.0 copy-start.23
  0.7 0.0 copy-start.8
  0.7 0.0 copy-start.7
  0.7 1.8 fusion.63
  2.5 2.5 collective-permute-start
  5.0 5.3 %collective-permute-start.1 = (bf16[128,512]{1,0:T(8,128)(2,1)S(1)}, bf16[128,512]{1,0:T(8,128)(2,1)S(1)}, u32[]{:S(2)}, u32[]{:S(2)}) collective-permute-start(bf16[128,512]{1,0:T(8,128)(2,1)S(1)} %get-tuple-element.25), channel_id=1, source_target_pairs={{1,0},{2,1},{3,2},{4,3},{5,4},{6,5},{7,6},{8,7},{9,8},{10,9},{11,1... | collective-permute-start | bytes 393224 | tf_op jit(solution)/shard_map/ppermute | solution.py:17
  10.3 2.3 stack.2
  12.6 6.2 %all-to-all-start = ((bf16[128,16,512]{2,1,0:T(8,128)(2,1)}), bf16[128,16,512]{2,1,0:T(8,128)(2,1)}, u32[]{:S(2)}, u32[]{:S(2)}) async-start(bf16[128,16,512]{2,1,0:T(8,128)(2,1)} %stack.2), calls=%async_computation | async-start | bytes 4194304 | tf_op jit(solution)/shard_map/all_to_all | solution.py:94
  18.8 0.6 pad_clamp_fusion.3
  19.4 0.6 pad_clamp_fusion.1
  20.0 0.2 copy.50
  20.3 1.0 copy.51
  21.3 6.4 %copy.49 = bf16[4096,512]{0,1:T(8,128)(2,1)} copy(bf16[4096,512]{1,0:T(8,128)(2,1)} %param.26) | data formatting | bytes 8388608 | tf_op args[2]
  27.6 0.6 pad_clamp_fusion.2
  28.3 0.6 fusion.49
  28.9 6.6 %maximum_convert_fusion = f32[5120,512]{0,1:T(8,128)} fusion(bf16[512,512]{0,1:T(8,128)(2,1)} %copy.51, bf16[512,512]{0,1:T(8,128)(2,1)S(1)} %copy.50, bf16[4096,512]{0,1:T(8,128)(2,1)} %copy.49), kind=kLoop, calls=%fused_computation.32 | loop fusion | flops 15728640 | bytes 15728640 | tf_op jit(solution)/shard_map/convert_element_type | solution.py:106
  35.5 0.6 pad_clamp_fusion
  36.1 1.3 copy.48
  38.0 2.8 %gather_fusion.5 = bf16[512,512]{1,0:T(8,128)(2,1)} fusion(bf16[1024,512]{1,0:T(8,128)(2,1)S(1)} %copy-done.2, s32[1024]{0:T(1024)} %pad_clamp_fusion), kind=kCustom, calls=%fused_computation.5 | custom fusion | bytes 1050624 | tf_op jit(solution)/shard_map/gather | solution.py:104
  40.8 2.8 %gather_fusion.2 = bf16[512,512]{1,0:T(8,128)(2,1)} fusion(bf16[1024,512]{1,0:T(8,128)(2,1)S(1)} %copy-done.2, s32[1024]{0:T(1024)} %pad_clamp_fusion.3), kind=kCustom, calls=%fused_computation.2 | custom fusion | bytes 1050624 | tf_op jit(solution)/shard_map/gather | solution.py:102
  43.6 18.6 %gather_fusion.1 = bf16[4096,512]{1,0:T(8,128)(2,1)} fusion(bf16[1024,512]{1,0:T(8,128)(2,1)S(1)} %copy-done.2, s32[4096]{0:T(1024)} %fusion.49), kind=kCustom, calls=%fused_computation.1 | custom fusion | bytes 8404992 | tf_op jit(solution)/shard_map/gather | solution.py:100
  62.2 0.6 iota_compare_fusion
  62.8 1.2 pad_maximum_fusion
  64.0 19.0 %gather_fusion = bf16[4096,512]{1,0:T(8,128)(2,1)} fusion(bf16[1280,512]{1,0:T(8,128)(2,1)} %pad_maximum_fusion, s32[4096]{0:T(1024)S(1)} %fusion.48), kind=kCustom, calls=%fused_computation | custom fusion | bytes 8404992 | tf_op jit(solution)/shard_map/gather | solution.py:100
  83.0 0.0 copy-start.28
  83.0 4.5 %gather_fusion.4 = bf16[512,512]{1,0:T(8,128)(2,1)} fusion(bf16[2048,512]{1,0:T(8,128)(2,1)} %bitcast.1, s32[1024]{0:T(1024)S(1)} %copy-done.15), kind=kCustom, calls=%fused_computation.4 | custom fusion | bytes 1050624 | tf_op jit(solution)/shard_map/gather | solution.py:104
  87.6 4.5 %gather_fusion.3 = bf16[512,512]{1,0:T(8,128)(2,1)} fusion(bf16[2048,512]{1,0:T(8,128)(2,1)} %bitcast.1, s32[1024]{0:T(1024)S(1)} %copy-done.16), kind=kCustom, calls=%fused_computation.3 | custom fusion | bytes 1050624 | tf_op jit(solution)/shard_map/gather | solution.py:102
  92.1 0.0 copy-start.27
  92.1 27.5 %multiply_convert_fusion.clone.1.clone.4 = bf16[5120,512]{1,0:T(8,128)(2,1)} fusion(bf16[1536,512]{1,0:T(8,128)(2,1)S(1)} %copy-done, bf16[512,512]{1,0:T(8,128)(2,1)} %gather_fusion.5, bf16[512,512]{1,0:T(8,128)(2,1)} %gather_fusion.4, bf16[512,512]{1,0:T(8,128)(2,1)} %param.33, bf16[512,512]{1,0:T(8,128)(2,1)} %gather_fusion.3, ...), kind=kOutput, calls=%fused_computation.29.clone.clone.clone.clone.clone.1 | convolution fusion | flops 8210350080 | bytes 22546432 | tf_op jit(solution)/shard_map/dot_general | solution.py:35
  119.6 5.3 %add_reduce_fusion = (f32[5120]{0:T(1024)S(1)}, f32[5120,512]{0,1:T(8,128)S(1)}) fusion(f32[512]{0:T(512)S(1)} %copy-done.19, bf16[512,512]{1,0:T(8,128)(2,1)S(1)} %copy-done.27, bf16[5120,512]{1,0:T(8,128)(2,1)} %multiply_convert_fusion.clone.1.clone.4), kind=kOutput, calls=%fused_computation.30 | convolution fusion | flops 2689592320 | bytes 16275456 | tf_op jit(solution)/shard_map/dot_general | solution.py:37
  124.9 0.0 copy-start.5
  124.9 0.0 copy-start.25
  125.0 1.9 multiply_reduce_fusion
  126.9 0.2 copy-done.4
  127.1 0.1 copy-done.5
  127.2 3.1 %add_add_fusion = f32[5120,512]{0,1:T(8,128)S(1)} fusion(f32[5120,512]{0,1:T(8,128)S(1)} %get-tuple-element.27, f32[512]{0:T(512)S(1)} %copy-done.25, f32[512]{0:T(512)S(1)} %copy-done.26, f32[5120]{0:T(1024)S(1)} %add_rsqrt_fusion, f32[5120]{0:T(1024)S(1)} %broadcast_multiply_fusion, f32[512]{0:T(512)S(1)} %copy-done.19, bf16[512,512]{0,1:T(8,128)(2,1)S(1)} %copy-done.5, ...), kind=kLoop, calls=%fused_computation.27 | loop fusion | flops 31457280 | bytes 26261504 | tf_op jit(solution)/shard_map/add | solution.py:107
  130.3 3.8 %copy-done.3 = f32[5120,512]{0,1:T(8,128)} copy-done((f32[5120,512]{0,1:T(8,128)}, f32[5120,512]{0,1:T(8,128)S(1)}, u32[]{:S(2)}) %copy-start.3) | copy-done | bytes 10485784
  134.1 1.1 fusion.62
  135.3 2.5 %copy.54 = f32[512,512]{1,0:T(8,128)} copy(f32[512,512]{0,1:T(8,128)} %get-tuple-element.22) | data formatting | bytes 2097152 | tf_op jit(solution)/shard_map/slice | solution.py:112
  137.8 6.5 %scatter_custom_fusion.2 = f32[2048,512]{1,0:T(8,128)} fusion(s32[512]{0:T(512)} %param.32, f32[512,512]{1,0:T(8,128)} %copy.54, f32[]{:T(128)} %constant.9.clone.1), kind=kCustom, calls=%fused_computation.40 | custom fusion | flops 262144 | bytes 4194816 | tf_op jit(solution)/shard_map/scatter-add | solution.py:126
  144.3 6.1 %all-to-all-start.1 = ((f32[4,1,32,16,512]{4,3,2,1,0:T(8,128)}), f32[4,1,32,16,512]{4,3,2,1,0:T(8,128)}, u32[]{:S(2)}, u32[]{:S(2)}) async-start(f32[4,1,32,16,512]{4,3,2,1,0:T(8,128)} %bitcast.18), calls=%async_computation.1 | async-start | bytes 8388608 | tf_op jit(solution)/shard_map/all_to_all | solution.py:30
  150.3 9.5 %broadcast_select_fusion = f32[4096,512]{0,1:T(8,128)} fusion(pred[4096]{0:T(1024)(128)(4,1)S(1)} %copy-done.11, f32[5120,512]{0,1:T(8,128)} %maximum_convert_fusion, f32[5120,512]{0,1:T(8,128)} %copy-done.3), kind=kLoop, calls=%fused_computation.34 | loop fusion | flops 4194304 | bytes 25169920 | tf_op jit(solution)/shard_map/jit(_where)/select_n | solution.py:115
  159.8 1.4 copy.53
  161.2 5.7 %scatter_custom_fusion.1 = f32[1024,512]{1,0:T(8,128)} fusion(s32[512]{0:T(512)} %param.35, f32[512,512]{1,0:T(8,128)} %copy.53, f32[]{:T(128)} %constant.9.clone.1), kind=kCustom, calls=%fused_computation.53 | custom fusion | flops 262144 | bytes 2097664 | tf_op jit(solution)/shard_map/scatter-add | solution.py:118
  166.9 9.1 %copy.52 = f32[4096,512]{1,0:T(8,128)} copy(f32[4096,512]{0,1:T(8,128)} %broadcast_select_fusion) | data formatting | bytes 16777216 | tf_op jit(solution)/shard_map/jit(_where)/select_n | solution.py:115
  176.0 26.6 %scatter_custom_fusion = f32[1024,512]{1,0:T(8,128)} fusion(s32[4096]{0:T(1024)} %param.28, f32[4096,512]{1,0:T(8,128)} %copy.52, f32[]{:T(128)} %constant.9.clone.1), kind=kCustom, calls=%fused_computation.55 | custom fusion | flops 2097152 | bytes 2097664 | tf_op jit(solution)/shard_map/scatter-add | solution.py:114
  202.6 2.6 %add_convert_fusion.1 = bf16[1024,512]{1,0:T(8,128)(2,1)S(1)} fusion(f32[1024,512]{1,0:T(8,128)} %scatter_custom_fusion, f32[1024,512]{1,0:T(8,128)} %scatter_custom_fusion.1), kind=kLoop, calls=%fused_computation.45 | loop fusion | flops 1048576 | bytes 5242880 | tf_op jit(solution)/shard_map/convert_element_type | solution.py:119
  205.2 4.6 %add_reduce_fusion.1 = (f32[1024]{0:T(1024)S(1)}, f32[1024,512]{0,1:T(8,128)}) fusion(f32[512]{0:T(512)S(1)} %copy-done.12, bf16[512,512]{1,0:T(8,128)(2,1)S(1)} %copy-done.9, bf16[1024,512]{1,0:T(8,128)(2,1)} %param.42, bf16[1024,512]{1,0:T(8,128)(2,1)S(1)} %add_convert_fusion.1, bf16[1024,512]{1,0:T(8,128)(2,1)S(1)} %copy-done.2, f32[512]{0:T(512)S(1)} %copy-done.20), kind=kOutput, calls=%fused_computation.46 | convolution fusion | flops 1619000320 | bytes 5775360 | tf_op jit(solution)/shard_map/dot_general | solution.py:37
  209.9 8.5 %fusion.23 = bf16[4096,512]{0,1:T(8,128)(2,1)} fusion(f32[5120,512]{0,1:T(8,128)} %maximum_convert_fusion, f32[5120,512]{0,1:T(8,128)} %copy-done.3, pred[4096]{0:T(1024)(128)(4,1)S(1)} %copy-done.11), kind=kLoop, calls=%fused_computation.35 | loop fusion | flops 2097152 | bytes 12587008 | tf_op jit(solution)/shard_map/convert_element_type | solution.py:139
  218.3 3.8 %reduce_sum.76 = f32[32,16,512]{2,1,0:T(8,128)} reduce(f32[4,1,32,16,512]{4,3,2,1,0:T(8,128)} %all-to-all-done.1, f32[]{:T(128)} %constant.9.clone.1), dimensions={0,1}, to_apply=%region_7.8 | reduce | flops 786432 | bytes 5242884 | tf_op jit(solution)/shard_map/reduce_sum | solution.py:31
  222.1 8.0 %all-to-all-start.2 = ((f32[32,1,1,16,512]{4,3,2,1,0:T(8,128)}), f32[32,1,1,16,512]{4,3,2,1,0:T(8,128)}, u32[]{:S(2)}, u32[]{:S(2)}) async-start(f32[32,1,1,16,512]{4,3,2,1,0:T(8,128)} %bitcast.4), calls=%async_computation.2 | async-start | bytes 2097152 | tf_op jit(solution)/shard_map/all_to_all | solution.py:30
  230.0 1.7 fusion.61
  231.7 1.0 copy.59
  232.7 1.0 copy.58
  233.7 6.5 %copy.57 = bf16[4096,512]{1,0:T(8,128)(2,1)} copy(bf16[4096,512]{0,1:T(8,128)(2,1)} %fusion.23) | data formatting | bytes 8388608
  240.2 1.9 multiply_reduce_fusion.1
  242.2 0.0 copy-start.1
  242.2 3.3 %add_convert_fusion = bf16[1024,512]{0,1:T(8,128)(2,1)} fusion(bf16[1024,512]{0,1:T(8,128)(2,1)S(1)} %copy-done.6, f32[1024,512]{0,1:T(8,128)} %get-tuple-element.29, f32[512]{0:T(512)S(1)} %copy-done.17, f32[512]{0:T(512)S(1)} %copy-done.18, f32[1024]{0:T(1024)S(1)} %add_rsqrt_fusion.1, f32[1024]{0:T(1024)S(1)} %broadcast_multiply_fusion.1, ...), kind=kLoop, calls=%fused_computation.42 | loop fusion | flops 4194304 | bytes 4208640 | tf_op jit(solution)/shard_map/convert_element_type | solution.py:137
  245.6 2.3 copy.56
  247.8 1.3 reduce_sum.77
  249.1 1.7 fusion.68
  250.9 0.2 multiply_reduce_fusion.2
  251.1 0.7 add_convert_fusion.2
  (62 shorter events, 0.2 us)
Async XLA Ops:
  0.6 91.5 %copy-start = (bf16[1536,512]{1,0:T(8,128)(2,1)S(1)}, bf16[1536,512]{1,0:T(8,128)(2,1)}, u32[]{:S(2)}) copy-start(bf16[1536,512]{1,0:T(8,128)(2,1)} %param.36) | copy-start | bytes 4718596
  0.6 18.1 %copy-start.21 = (s32[512]{0:T(512)S(1)}, s32[512]{0:T(512)}, u32[]{:S(2)}) copy-start(s32[512]{0:T(512)} %param.31) | copy-start | bytes 6148
  0.7 18.8 %copy-start.22 = (s32[512]{0:T(512)S(1)}, s32[512]{0:T(512)}, u32[]{:S(2)}) copy-start(s32[512]{0:T(512)} %param.34) | copy-start | bytes 6148
  0.7 19.4 %copy-start.23 = (s32[512]{0:T(512)S(1)}, s32[512]{0:T(512)}, u32[]{:S(2)}) copy-start(s32[512]{0:T(512)} %param.32) | copy-start | bytes 6148
  0.7 19.3 %copy-start.8 = (bf16[512,512]{1,0:T(8,128)(2,1)S(1)}, bf16[512,512]{1,0:T(8,128)(2,1)}, u32[]{:S(2)}) copy-start(bf16[512,512]{1,0:T(8,128)(2,1)} %param.30) | copy-start | bytes 1572868
  0.7 19.6 %copy-start.7 = (bf16[512,512]{1,0:T(8,128)(2,1)S(1)}, bf16[512,512]{1,0:T(8,128)(2,1)}, u32[]{:S(2)}) copy-start(bf16[512,512]{1,0:T(8,128)(2,1)} %param.33) | copy-start | bytes 1572868
  2.5 60.2 %collective-permute-start = (bf16[128,512]{1,0:T(8,128)(2,1)}, bf16[128,512]{1,0:T(8,128)(2,1)S(1)}, u32[]{:S(2)}, u32[]{:S(2)}) collective-permute-start(bf16[128,512]{1,0:T(8,128)(2,1)} %get-tuple-element.24), channel_id=1, source_target_pairs={{0,1},{1,2},{2,3},{3,4},{4,5},{5,6},{6,7},{7,8},{8,9},{9,10},{10,1... | collective-permute-start | bytes 393224 | tf_op jit(solution)/shard_map/ppermute | solution.py:16
  5.0 57.8 %collective-permute-start.1 = (bf16[128,512]{1,0:T(8,128)(2,1)S(1)}, bf16[128,512]{1,0:T(8,128)(2,1)S(1)}, u32[]{:S(2)}, u32[]{:S(2)}) collective-permute-start(bf16[128,512]{1,0:T(8,128)(2,1)S(1)} %get-tuple-element.25), channel_id=1, source_target_pairs={{1,0},{2,1},{3,2},{4,3},{5,4},{6,5},{7,6},{8,7},{9,8},{10,9},{11,1... | collective-permute-start | bytes 393224 | tf_op jit(solution)/shard_map/ppermute | solution.py:17
  12.6 70.4 %all-to-all-start = ((bf16[128,16,512]{2,1,0:T(8,128)(2,1)}), bf16[128,16,512]{2,1,0:T(8,128)(2,1)}, u32[]{:S(2)}, u32[]{:S(2)}) async-start(bf16[128,16,512]{2,1,0:T(8,128)(2,1)} %stack.2), calls=%async_computation | async-start | bytes 4194304 | tf_op jit(solution)/shard_map/all_to_all | solution.py:94
  21.3 7.0 %copy-start.24 = (s32[512]{0:T(512)S(1)}, s32[512]{0:T(512)}, u32[]{:S(2)}) copy-start(s32[512]{0:T(512)} %param.35) | copy-start | bytes 6148
  21.3 7.0 %copy-start.13 = (s32[4096]{0:T(1024)S(1)}, s32[4096]{0:T(1024)}, u32[]{:S(2)}) copy-start(s32[4096]{0:T(1024)} %param.27) | copy-start | bytes 49156
  21.3 7.0 %copy-start.14 = (s32[4096]{0:T(1024)S(1)}, s32[4096]{0:T(1024)}, u32[]{:S(2)}) copy-start(s32[4096]{0:T(1024)} %param.28) | copy-start | bytes 49156
  28.9 7.2 %copy-start.2 = (bf16[1024,512]{1,0:T(8,128)(2,1)S(1)}, bf16[1024,512]{1,0:T(8,128)(2,1)}, u32[]{:S(2)}) copy-start(bf16[1024,512]{1,0:T(8,128)(2,1)} %param.24) | copy-start | bytes 3145732
  64.0 19.0 %copy-start.15 = (s32[1024]{0:T(1024)S(1)}, s32[1024]{0:T(1024)}, u32[]{:S(2)}) copy-start(s32[1024]{0:T(1024)} %pad_clamp_fusion.1) | copy-start | bytes 12292
  83.0 4.6 %copy-start.16 = (s32[1024]{0:T(1024)S(1)}, s32[1024]{0:T(1024)}, u32[]{:S(2)}) copy-start(s32[1024]{0:T(1024)} %pad_clamp_fusion.2) | copy-start | bytes 12292
  83.0 9.1 %copy-start.28 = (f32[512]{0:T(512)S(1)}, f32[512]{0:T(512)}, u32[]{:S(2)}) copy-start(f32[512]{0:T(512)} %param.37) | copy-start | bytes 6148
  92.1 27.5 %copy-start.19 = (f32[512]{0:T(512)S(1)}, f32[512]{0:T(512)}, u32[]{:S(2)}) copy-start(f32[512]{0:T(512)} %param.39) | copy-start | bytes 6148
  92.1 27.5 %copy-start.27 = (bf16[512,512]{1,0:T(8,128)(2,1)S(1)}, bf16[512,512]{1,0:T(8,128)(2,1)}, u32[]{:S(2)}) copy-start(bf16[512,512]{1,0:T(8,128)(2,1)} %param.38) | copy-start | bytes 1572868
  124.9 2.2 copy-start.4
  124.9 2.3 copy-start.5
  124.9 2.3 copy-start.25
  124.9 2.3 copy-start.26
  130.3 3.8 %copy-start.3 = (f32[5120,512]{0,1:T(8,128)}, f32[5120,512]{0,1:T(8,128)S(1)}, u32[]{:S(2)}) copy-start(f32[5120,512]{0,1:T(8,128)S(1)} %add_add_fusion) | copy-start | bytes 31457284
  144.3 6.1 %copy-start.11 = (pred[4096]{0:T(1024)(128)(4,1)S(1)}, pred[4096]{0:T(1024)(128)(4,1)}, u32[]{:S(2)}) copy-start(pred[4096]{0:T(1024)(128)(4,1)} %iota_compare_fusion) | copy-start | bytes 12292
  144.3 74.1 %all-to-all-start.1 = ((f32[4,1,32,16,512]{4,3,2,1,0:T(8,128)}), f32[4,1,32,16,512]{4,3,2,1,0:T(8,128)}, u32[]{:S(2)}, u32[]{:S(2)}) async-start(f32[4,1,32,16,512]{4,3,2,1,0:T(8,128)} %bitcast.18), calls=%async_computation.1 | async-start | bytes 8388608 | tf_op jit(solution)/shard_map/all_to_all | solution.py:30
  176.0 29.2 %copy-start.9 = (bf16[512,512]{1,0:T(8,128)(2,1)S(1)}, bf16[512,512]{1,0:T(8,128)(2,1)}, u32[]{:S(2)}) copy-start(bf16[512,512]{1,0:T(8,128)(2,1)} %param.44) | copy-start | bytes 1572868
  176.0 29.2 %copy-start.12 = (f32[512]{0:T(512)S(1)}, f32[512]{0:T(512)}, u32[]{:S(2)}) copy-start(f32[512]{0:T(512)} %param.45) | copy-start | bytes 6148
  176.0 29.2 %copy-start.20 = (f32[512]{0:T(512)S(1)}, f32[512]{0:T(512)}, u32[]{:S(2)}) copy-start(f32[512]{0:T(512)} %param.43) | copy-start | bytes 6148
  222.1 25.8 %all-to-all-start.2 = ((f32[32,1,1,16,512]{4,3,2,1,0:T(8,128)}), f32[32,1,1,16,512]{4,3,2,1,0:T(8,128)}, u32[]{:S(2)}, u32[]{:S(2)}) async-start(f32[32,1,1,16,512]{4,3,2,1,0:T(8,128)} %bitcast.4), calls=%async_computation.2 | async-start | bytes 2097152 | tf_op jit(solution)/shard_map/all_to_all | solution.py:30
  233.7 8.5 %copy-start.6 = (bf16[1024,512]{0,1:T(8,128)(2,1)S(1)}, bf16[1024,512]{0,1:T(8,128)(2,1)}, u32[]{:S(2)}) copy-start(bf16[1024,512]{0,1:T(8,128)(2,1)} %copy.48) | copy-start | bytes 3145732
  233.7 8.5 %copy-start.17 = (f32[512]{0:T(512)S(1)}, f32[512]{0:T(512)}, u32[]{:S(2)}) copy-start(f32[512]{0:T(512)} %param.47) | copy-start | bytes 6148
  233.7 8.5 %copy-start.18 = (f32[512]{0:T(512)S(1)}, f32[512]{0:T(512)}, u32[]{:S(2)}) copy-start(f32[512]{0:T(512)} %param.46) | copy-start | bytes 6148
  242.2 7.0 %copy-start.10 = (bf16[16,512]{1,0:T(8,128)(2,1)S(1)}, bf16[16,512]{1,0:T(8,128)(2,1)}, u32[]{:S(2)}) copy-start(bf16[16,512]{1,0:T(8,128)(2,1)} %param.25) | copy-start | bytes 49156
  242.2 9.6 %copy-start.1 = (bf16[1536,512]{1,0:T(8,128)(2,1)S(1)}, bf16[1536,512]{1,0:T(8,128)(2,1)}, u32[]{:S(2)}) copy-start(bf16[1536,512]{1,0:T(8,128)(2,1)} %param.36) | copy-start | bytes 4718596
